TPU v7x, 32 devices: a whole 2x2x4 slice. The times are simulated.
32 devices in a mesh: groups: 2 (over y), seg: 4 (over z), bin: 4 (over x, core).
Axes of the slice: x: 2, y: 2, z: 4, core: 2. Of those that a mesh axis runs over, the one named last changes fastest.
Arguments:
- start_factors: float32 [4096, 128], P(('groups', 'seg', 'bin')), parts along dimension 0, may hold values from -6 to 6
- bin_factors: bfloat16 [8192, 128], P(('groups', 'bin')), parts along dimension 0, may hold values from -0.5 to 0.5
- tile_speed: bfloat16 [8, 4, 12, 128, 128], P(('groups', 'seg'), 'bin'), parts along dimension 0, may hold values from -6 to 6
- tile_weight: bfloat16 [8, 4, 12, 128, 128], P(('groups', 'seg'), 'bin'), parts along dimension 0, may hold values from 0.099609375 to 2
- tile_cells: int32 [8, 4, 12, 2], P(('groups', 'seg'), 'bin'), parts along dimension 0, may hold values from 0 to 7, as said below
- tile_count: int32 [8, 4], P(('groups', 'seg'), 'bin'), parts along dimension 0, may hold values from 1 to 12, as said below
- inner_pairs: int32 [8, 4, 2, 2], P(('groups', 'seg'), 'bin'), parts along dimension 0, may hold values from 0 to 3, as said below
- inner_weight: float32 [8, 4, 2, 128, 128], P(('groups', 'seg'), 'bin'), parts along dimension 0, may hold values from 0 to 0.00390625
- face_rows: int32 [8, 4, 2, 256], P(('groups', 'seg'), 'bin'), parts along dimension 0, may hold values from 0 to 511, as said below
- face_count: int32 [8, 4, 2], P(('groups', 'seg'), 'bin'), parts along dimension 0, may hold values from 128 to 256, as said below
- face_weight: float32 [8, 4, 256, 256], P(('groups', 'seg'), 'bin'), parts along dimension 0, may hold values from 0 to 0.00390625
Outputs:
- solution_factors: float32 [4096, 128], P(('groups', 'seg', 'bin')), parts along dimension 0
- residual: float32 [4096, 128], P(('groups', 'seg', 'bin')), parts along dimension 0
There are 2 independent parts, one for each index of `groups`. A program takes and returns all parts, laid end to end along the dimension named above; each array names one. Nothing has to cross between parts.
Inputs may be any that keep to these rules, and one draw needn't show every extreme that they name: `tile_cells`: the 12 slots of one device name different pairs; the first entry is a segment block of the partition, the second a bin block of the device's bins. `tile_count`: some device of every draw has all 12 slots live. `inner_pairs`: the two blocks of a pair differ; both are segment blocks of the partition. `face_rows`: row numbers within the partition, different within each face list. `face_count`: some face list of every draw has all 256 rows live.
All inputs are finite; a program needn't handle non-finite values.
Results may differ from a plain program's by a relative error of at most 0.0024.
Values sent between devices are 32-bit elements; how exact they have to be, the bound alone decides.
No kernel may reach another device: no remote copies, remote signals or barrier semaphores. Data moves between devices by JAX's collectives and lax.ppermute only.
A program may use at most 64 MiB of HBM per device.

v0:
```python
import jax
import jax.numpy as jnp
from jax import lax
from jax.sharding import PartitionSpec as P

ITERS = 2
highest = lax.Precision.HIGHEST
ridge_weight = 0.5


def from_behind(x, axis, by):
    devices = lax.axis_size(axis)
    pairs = [(i, i + by) for i in range(devices) if 0 <= i + by < devices]
    return lax.ppermute(x, axis, pairs)


def shards(
    start_factors,
    bin_factors,
    tile_speed,
    tile_weight,
    tile_cells,
    tile_count,
    inner_pairs,
    inner_weight,
    face_rows,
    face_count,
    face_weight,
):
    speeds = tile_speed[0, 0]
    weights = tile_weight[0, 0]
    cells = tile_cells[0, 0]
    n_tiles = speeds.shape[0]
    tile_size = speeds.shape[1]
    own_rows = start_factors.shape[0]
    width = start_factors.shape[1]
    part_rows = own_rows * lax.axis_size("bin")
    part_blocks = part_rows // tile_size
    block_ids = jnp.arange(part_blocks, dtype=jnp.int32)
    live_tiles = (jnp.arange(n_tiles, dtype=jnp.int32) < tile_count[0, 0]).astype(jnp.float32)
    tile_bins = bin_factors.reshape(-1, tile_size, width)[cells[:, 1]]
    bins_wide = tile_bins.astype(jnp.float32)
    tile_gain = weights.astype(jnp.float32) * live_tiles[:, None, None]
    tile_onehot = (cells[:, 0][:, None] == block_ids[None, :]).astype(jnp.float32)
    weighted = (weights.astype(jnp.float32) * speeds.astype(jnp.float32)).astype(jnp.bfloat16)
    rhs_terms = jnp.einsum("kij,kjr->kir", weighted, tile_bins, preferred_element_type=jnp.float32)
    rhs_terms = rhs_terms * live_tiles[:, None, None]
    rhs_part = jnp.einsum("kb,kir->bir", tile_onehot, rhs_terms, precision=highest).reshape(
        part_rows, width
    )
    pairs = inner_pairs[0, 0]
    pair_weight = inner_weight[0, 0]
    left_onehot = (pairs[:, 0][:, None] == block_ids[None, :]).astype(jnp.float32)
    right_onehot = (pairs[:, 1][:, None] == block_ids[None, :]).astype(jnp.float32)
    left_degree = pair_weight.sum(2)
    right_degree = pair_weight.sum(1)
    rows_low = face_rows[0, 0, 0]
    rows_up = face_rows[0, 0, 1]
    face_slots = jnp.arange(rows_low.shape[0], dtype=jnp.int32)
    mask_low = (face_slots < face_count[0, 0, 0]).astype(jnp.float32)
    mask_up = (face_slots < face_count[0, 0, 1]).astype(jnp.float32)
    upper_count = face_count[0, 0, 1:2]
    face_block = face_weight[0, 0]

    def apply_local(whole_rows):
        blocks = whole_rows.reshape(part_blocks, tile_size, width)
        picked = blocks[cells[:, 0]]
        scores = jnp.einsum("kir,kjr->kij", picked, bins_wide, precision=highest) * tile_gain
        pulled = jnp.einsum("kij,kjr->kir", scores, bins_wide, precision=highest)
        left = blocks[pairs[:, 0]]
        right = blocks[pairs[:, 1]]
        to_left = left_degree[..., None] * left - jnp.einsum(
            "kij,kjr->kir", pair_weight, right, precision=highest
        )
        to_right = right_degree[..., None] * right - jnp.einsum(
            "kij,kir->kjr", pair_weight, left, precision=highest
        )
        summed = jnp.einsum("kb,kir->bir", tile_onehot, pulled, precision=highest)
        summed = summed + jnp.einsum("kb,kir->bir", left_onehot, to_left, precision=highest)
        summed = summed + jnp.einsum("kb,kir->bir", right_onehot, to_right, precision=highest)
        summed = summed.reshape(part_rows, width)
        own_face = whole_rows[rows_low] * mask_low[:, None]
        upper_face = whole_rows[rows_up] * mask_up[:, None]
        lower_face, lower_count = from_behind((upper_face, upper_count), "seg", 1)
        lower_mask = (face_slots < lower_count[0]).astype(jnp.float32)
        coupling = face_block * mask_low[:, None] * lower_mask[None, :]
        own_term = coupling.sum(1)[:, None] * own_face - jnp.dot(
            coupling, lower_face, precision=highest
        )
        answer = coupling.sum(0)[:, None] * lower_face - jnp.dot(
            coupling.T, own_face, precision=highest
        )
        returned = from_behind(answer, "seg", -1)
        return summed.at[rows_low].add(own_term).at[rows_up].add(returned)

    def reduce_rows(partial_value):
        reduced = lax.psum_scatter(partial_value, "bin", scatter_dimension=0, tiled=True)
        return reduced

    def spread(vector):
        whole_rows = lax.all_gather(vector, "bin", axis=0, tiled=True)
        return whole_rows

    def fold_sum(values):
        folded = lax.psum((values[0], values[1]), ("seg", "bin"))
        return folded

    def image_of(vector):
        return reduce_rows(apply_local(spread(vector))) + ridge_weight * vector

    start_whole = lax.all_gather(start_factors, "bin", axis=0, tiled=True)
    residual = reduce_rows(rhs_part - apply_local(start_whole)) - ridge_weight * start_factors
    solution = start_factors
    images = image_of(residual)
    norm_now, product = fold_sum((jnp.sum(residual * residual), jnp.sum(residual * images)))
    step_size = norm_now / product
    direction = residual
    along = images
    for iteration in range(ITERS):
        solution = solution + step_size * direction
        residual = residual - step_size * along
        if iteration + 1 < ITERS:
            images = image_of(residual)
            norm_next, product = fold_sum(
                (jnp.sum(residual * residual), jnp.sum(residual * images))
            )
            beta_ratio = norm_next / norm_now
            step_size = norm_next / (product - beta_ratio * norm_next / step_size)
            direction = residual + beta_ratio * direction
            along = images + beta_ratio * along
            norm_now = norm_next
    outputs = (solution, residual)
    return outputs


def solution(mesh):
    return jax.shard_map(
        shards,
        mesh=mesh,
        in_specs=(
            P(("groups", "seg", "bin"), None),
            P(("groups", "bin"), None),
            P(("groups", "seg"), "bin", None, None, None),
            P(("groups", "seg"), "bin", None, None, None),
            P(("groups", "seg"), "bin", None, None),
            P(("groups", "seg"), "bin"),
            P(("groups", "seg"), "bin", None, None),
            P(("groups", "seg"), "bin", None, None, None),
            P(("groups", "seg"), "bin", None, None),
            P(("groups", "seg"), "bin", None),
            P(("groups", "seg"), "bin", None, None),
        ),
        out_specs=(P(("groups", "seg", "bin"), None), P(("groups", "seg", "bin"), None)),
        check_vma=False,
    )
```

profile of v0, /device:TPU:0, one launch (start us, length us, event | category | flops | bytes accessed | tf_op | source)
XLA Modules:
  0.0 242.0 jit_solution(7704379374900717921)
XLA Ops:
  7.2 1.4 fusion.76
  8.6 5.6 %collective-permute-start = (s32[1]{0:T(128)}, s32[1]{0:T(128)}, u32[]{:S(2)}, u32[]{:S(2)}) collective-permute-start(s32[1]{0:T(128)} %bitcast.23), channel_id=1, source_target_pairs={{0,4},{4,8},{8,12},{1,5},{5,9},{9,13},{2,6},{6,10},{10,14},{3,7},{... | collective-permute-start | bytes 20 | tf_op jit(solution)/shard_map/ppermute | solution.py:14
  14.2 6.0 %all_gather.9 = f32[512,128]{1,0:T(8,128)S(1)} all-gather(f32[128,128]{1,0:T(8,128)} %param.11), channel_id=1, replica_groups=mesh['groups'=2,'seg'=4,'bin'=4] {'bin'}, dimensions={0}, use_global_device_ids=true | all-gather | bytes 327680 | tf_op jit(solution)/shard_map/all_gather | solution.py:111
  20.2 0.7 compare_convert_fusion
  20.9 0.7 gather_fusion.5
  21.7 3.0 %collective-permute-start.1 = (f32[256,128]{1,0:T(8,128)S(1)}, f32[256,128]{1,0:T(8,128)S(1)}, u32[]{:S(2)}, u32[]{:S(2)}) collective-permute-start(f32[256,128]{1,0:T(8,128)S(1)} %broadcast_multiply_fusion.2), channel_id=1, source_target_pairs={{0,4},{4,8},{8,12},{1,5},{5,9},{9,13},{2,6},{6,10},{10,14},{3,7},{... | collective-permute-start | bytes 393224 | tf_op jit(solution)/shard_map/ppermute | solution.py:14
  25.5 0.6 gather_fusion.1
  26.1 0.6 gather_fusion
  27.1 1.0 convolution_multiply_fusion.3
  28.6 0.7 copy-done.10
  29.5 0.6 gather_fusion.2
  30.0 0.6 gather_fusion.3
  32.2 0.9 convolution_add_fusion.2
  33.2 0.5 convolution_add_fusion.5
  33.7 0.7 compare_convert_fusion.2
  34.4 0.7 gather_fusion.4
  35.7 0.9 fusion.9
  36.6 0.6 compare_convert_fusion.1
  37.7 0.7 multiply_subtract_fusion.2
  38.4 1.3 collective-permute-start.2
  40.1 2.0 scatter_fusion
  42.2 3.6 %collective-permute-done.2 = f32[256,128]{1,0:T(8,128)S(1)} collective-permute-done((f32[256,128]{1,0:T(8,128)S(1)}, f32[256,128]{1,0:T(8,128)S(1)}, u32[]{:S(2)}, u32[]{:S(2)}) %collective-permute-start.2) | collective-permute-done | bytes 131104 | tf_op jit(solution)/shard_map/ppermute | solution.py:14
  45.8 2.0 scatter_fusion.1
  47.8 0.7 bitcast_subtract_fusion
  48.6 19.4 %reduce-scatter.4.cloned.1.call-done = f32[128,128]{1,0:T(8,128)} async-done(((f32[512,128]{1,0:T(8,128)}), f32[128,128]{1,0:T(8,128)}) %reduce-scatter.4.cloned.1.call-update) | async-done | bytes 65552 | tf_op jit(solution)/shard_map/reduce_scatter | solution.py:97
  68.0 0.8 multiply_subtract_fusion.5
  68.9 5.8 %all_gather.10 = f32[512,128]{1,0:T(8,128)S(1)} all-gather(f32[128,128]{1,0:T(8,128)S(1)} %multiply_subtract_fusion.5), channel_id=1, replica_groups=mesh['groups'=2,'seg'=4,'bin'=4] {'bin'}, dimensions={0}, use_global_device_ids=true | all-gather | bytes 327680 | tf_op jit(solution)/shard_map/all_gather | solution.py:101
  74.6 0.7 gather_fusion.10
  75.4 0.7 gather_fusion.9
  76.1 0.6 gather_fusion.7
  76.7 0.6 gather_fusion.8
  77.2 0.6 gather_fusion.6
  78.6 3.6 %collective-permute-start.3 = (f32[256,128]{1,0:T(8,128)S(1)}, f32[256,128]{1,0:T(8,128)S(1)}, u32[]{:S(2)}, u32[]{:S(2)}) collective-permute-start(f32[256,128]{1,0:T(8,128)S(1)} %broadcast_multiply_fusion.1), channel_id=1, source_target_pairs={{0,4},{4,8},{8,12},{1,5},{5,9},{9,13},{2,6},{6,10},{10,14},{3,7},{... | collective-permute-start | bytes 393224 | tf_op jit(solution)/shard_map/ppermute | solution.py:14
  82.2 0.9 convolution_multiply_fusion.2
  84.2 0.9 convolution_add_fusion.1
  85.1 0.5 convolution_add_fusion.4
  85.7 0.7 multiply_subtract_fusion.1
  86.4 1.3 collective-permute-start.4
  88.1 2.0 scatter_fusion.2
  90.2 3.6 %collective-permute-done.4 = f32[256,128]{1,0:T(8,128)S(1)} collective-permute-done((f32[256,128]{1,0:T(8,128)S(1)}, f32[256,128]{1,0:T(8,128)S(1)}, u32[]{:S(2)}, u32[]{:S(2)}) %collective-permute-start.4) | collective-permute-done | bytes 131104 | tf_op jit(solution)/shard_map/ppermute | solution.py:14
  93.7 2.0 scatter_fusion.3
  95.8 0.7 copy-done.2
  96.5 19.3 %reduce-scatter.6.cloned.1.call-done = f32[128,128]{1,0:T(8,128)} async-done(((f32[512,128]{1,0:T(8,128)}), f32[128,128]{1,0:T(8,128)}) %reduce-scatter.6.cloned.1.call-update) | async-done | bytes 65552 | tf_op jit(solution)/shard_map/reduce_scatter | solution.py:97
  115.9 1.5 multiply_reduce_fusion.2
  117.4 32.6 %all-reduce.1 = (f32[]{:T(128)}, f32[]{:T(128)}) all-reduce(f32[]{:T(128)} %get-tuple-element.9, f32[]{:T(128)} %get-tuple-element.8), channel_id=1, replica_groups=mesh['groups'=2,'seg'=4,'bin'=4] {'seg','bin'}, use_global_device_ids=true, to_apply=%region_8.0 | all-reduce | flops 2 | bytes 16 | tf_op jit(solution)/shard_map/psum | solution.py:105
  151.4 5.8 %all_gather.11 = f32[512,128]{1,0:T(8,128)S(1)} all-gather(f32[128,128]{1,0:T(8,128)S(1)} %multiply_subtract_fusion.4), channel_id=1, replica_groups=mesh['groups'=2,'seg'=4,'bin'=4] {'bin'}, dimensions={0}, use_global_device_ids=true | all-gather | bytes 327680 | tf_op jit(solution)/shard_map/all_gather | solution.py:101
  157.2 0.7 gather_fusion.15
  157.9 0.7 gather_fusion.14
  158.6 0.6 gather_fusion.12
  159.2 0.6 gather_fusion.13
  159.8 0.6 gather_fusion.11
  161.1 1.3 collective-permute-start.5
  162.5 1.0 convolution_multiply_fusion.1
  164.5 0.9 convolution_add_fusion
  166.0 0.7 multiply_subtract_fusion
  166.7 1.5 collective-permute-start.6
  168.6 2.0 scatter_fusion.4
  170.7 3.8 %collective-permute-done.6 = f32[256,128]{1,0:T(8,128)S(1)} collective-permute-done((f32[256,128]{1,0:T(8,128)S(1)}, f32[256,128]{1,0:T(8,128)S(1)}, u32[]{:S(2)}, u32[]{:S(2)}) %collective-permute-start.6) | collective-permute-done | bytes 131104 | tf_op jit(solution)/shard_map/ppermute | solution.py:14
  174.5 2.0 scatter_fusion.5
  176.5 0.7 copy-done.1
  177.2 18.7 %reduce-scatter.8.cloned.1.call-done = f32[128,128]{1,0:T(8,128)} async-done(((f32[512,128]{1,0:T(8,128)}), f32[128,128]{1,0:T(8,128)}) %reduce-scatter.8.cloned.1.call-update) | async-done | bytes 65552 | tf_op jit(solution)/shard_map/reduce_scatter | solution.py:97
  195.9 1.6 multiply_reduce_fusion
  197.5 32.7 %all-reduce = (f32[]{:T(128)}, f32[]{:T(128)}) all-reduce(f32[]{:T(128)} %get-tuple-element.7, f32[]{:T(128)} %get-tuple-element.6), channel_id=1, replica_groups=mesh['groups'=2,'seg'=4,'bin'=4] {'seg','bin'}, use_global_device_ids=true, to_apply=%region_15.0 | all-reduce | flops 2 | bytes 16 | tf_op jit(solution)/shard_map/psum | solution.py:105
  234.8 0.7 multiply_subtract_fusion.3
  (68 shorter events, 9.6 us)
Async XLA Ops:
  7.2 18.9 %copy-start = (bf16[1024,128]{1,0:T(8,128)(2,1)S(1)}, bf16[1024,128]{1,0:T(8,128)(2,1)}, u32[]{:S(2)}) copy-start(bf16[1024,128]{1,0:T(8,128)(2,1)} %param.12) | copy-start | bytes 786436
  7.2 60.8 %reduce-scatter.4.cloned.1.call-start = ((), (), s32[]{:S(2)}) async-start(), calls=%async_computation.3 | async-start | bytes 327680 | tf_op jit(solution)/shard_map/reduce_scatter | solution.py:97
  8.6 11.6 %copy-start.11 = (s32[1,1,2,256]{3,2,1,0:T(2,128)S(1)}, s32[1,1,2,256]{3,2,1,0:T(2,128)}, u32[]{:S(2)}) copy-start(s32[1,1,2,256]{3,2,1,0:T(2,128)} %param.19) | copy-start | bytes 6148
  8.6 28.0 %collective-permute-start = (s32[1]{0:T(128)}, s32[1]{0:T(128)}, u32[]{:S(2)}, u32[]{:S(2)}) collective-permute-start(s32[1]{0:T(128)} %bitcast.23), channel_id=1, source_target_pairs={{0,4},{4,8},{8,12},{1,5},{5,9},{9,13},{2,6},{6,10},{10,14},{3,7},{... | collective-permute-start | bytes 20 | tf_op jit(solution)/shard_map/ppermute | solution.py:14
  21.7 3.0 %copy-start.12 = (s32[1,1,12,2]{2,3,1,0:T(2,128)S(1)}, s32[1,1,12,2]{2,3,1,0:T(2,128)}, u32[]{:S(2)}) copy-start(s32[1,1,12,2]{2,3,1,0:T(2,128)} %param.15) | copy-start | bytes 292
  21.7 16.0 %collective-permute-start.1 = (f32[256,128]{1,0:T(8,128)S(1)}, f32[256,128]{1,0:T(8,128)S(1)}, u32[]{:S(2)}, u32[]{:S(2)}) collective-permute-start(f32[256,128]{1,0:T(8,128)S(1)} %broadcast_multiply_fusion.2), channel_id=1, source_target_pairs={{0,4},{4,8},{8,12},{1,5},{5,9},{9,13},{2,6},{6,10},{10,14},{3,7},{... | collective-permute-start | bytes 393224 | tf_op jit(solution)/shard_map/ppermute | solution.py:14
  26.1 1.0 copy-start.5
  28.5 0.7 copy-start.10
  30.0 0.9 copy-start.4
  34.4 1.0 copy-start.8
  36.6 1.0 copy-start.3
  38.4 7.4 %collective-permute-start.2 = (f32[256,128]{1,0:T(8,128)S(1)}, f32[256,128]{1,0:T(8,128)S(1)}, u32[]{:S(2)}, u32[]{:S(2)}) collective-permute-start(f32[256,128]{1,0:T(8,128)S(1)} %multiply_subtract_fusion.2), channel_id=1, source_target_pairs={{4,0},{8,4},{12,8},{5,1},{9,5},{13,9},{6,2},{10,6},{14,10},{7,3},{... | collective-permute-start | bytes 393224 | tf_op jit(solution)/shard_map/ppermute | solution.py:14
  48.5 19.5 %copy-start.6 = (f32[128,128]{1,0:T(8,128)S(1)}, f32[128,128]{1,0:T(8,128)}, u32[]{:S(2)}) copy-start(f32[128,128]{1,0:T(8,128)} %param.11) | copy-start | bytes 196612
  48.6 67.3 %reduce-scatter.6.cloned.1.call-start = ((), (), s32[]{:S(2)}) async-start(), calls=%async_computation.4 | async-start | bytes 327680 | tf_op jit(solution)/shard_map/reduce_scatter | solution.py:97
  78.6 7.1 %collective-permute-start.3 = (f32[256,128]{1,0:T(8,128)S(1)}, f32[256,128]{1,0:T(8,128)S(1)}, u32[]{:S(2)}, u32[]{:S(2)}) collective-permute-start(f32[256,128]{1,0:T(8,128)S(1)} %broadcast_multiply_fusion.1), channel_id=1, source_target_pairs={{0,4},{4,8},{8,12},{1,5},{5,9},{9,13},{2,6},{6,10},{10,14},{3,7},{... | collective-permute-start | bytes 393224 | tf_op jit(solution)/shard_map/ppermute | solution.py:14
  86.4 7.4 %collective-permute-start.4 = (f32[256,128]{1,0:T(8,128)S(1)}, f32[256,128]{1,0:T(8,128)S(1)}, u32[]{:S(2)}, u32[]{:S(2)}) collective-permute-start(f32[256,128]{1,0:T(8,128)S(1)} %multiply_subtract_fusion.1), channel_id=1, source_target_pairs={{4,0},{8,4},{12,8},{5,1},{9,5},{13,9},{6,2},{10,6},{14,10},{7,3},{... | collective-permute-start | bytes 393224 | tf_op jit(solution)/shard_map/ppermute | solution.py:14
  95.8 0.7 copy-start.2
  96.5 99.4 %reduce-scatter.8.cloned.1.call-start = ((), (), s32[]{:S(2)}) async-start(), calls=%async_computation.5 | async-start | bytes 327680 | tf_op jit(solution)/shard_map/reduce_scatter | solution.py:97
  115.8 35.5 %copy-start.7 = (f32[128,128]{1,0:T(8,128)S(1)}, f32[128,128]{1,0:T(8,128)}, u32[]{:S(2)}) copy-start(f32[128,128]{1,0:T(8,128)} %reduce-scatter.6.cloned.1.call-done) | copy-start | bytes 196612
  161.1 4.8 %collective-permute-start.5 = (f32[256,128]{1,0:T(8,128)S(1)}, f32[256,128]{1,0:T(8,128)S(1)}, u32[]{:S(2)}, u32[]{:S(2)}) collective-permute-start(f32[256,128]{1,0:T(8,128)S(1)} %broadcast_multiply_fusion), channel_id=1, source_target_pairs={{0,4},{4,8},{8,12},{1,5},{5,9},{9,13},{2,6},{6,10},{10,14},{3,7},{... | collective-permute-start | bytes 393224 | tf_op jit(solution)/shard_map/ppermute | solution.py:14
  166.7 7.8 %collective-permute-start.6 = (f32[256,128]{1,0:T(8,128)S(1)}, f32[256,128]{1,0:T(8,128)S(1)}, u32[]{:S(2)}, u32[]{:S(2)}) collective-permute-start(f32[256,128]{1,0:T(8,128)S(1)} %multiply_subtract_fusion), channel_id=1, source_target_pairs={{4,0},{8,4},{12,8},{5,1},{9,5},{13,9},{6,2},{10,6},{14,10},{7,3},{... | collective-permute-start | bytes 393224 | tf_op jit(solution)/shard_map/ppermute | solution.py:14
  176.5 0.7 copy-start.1
  195.9 38.9 %copy-start.9 = (f32[128,128]{1,0:T(8,128)S(1)}, f32[128,128]{1,0:T(8,128)}, u32[]{:S(2)}) copy-start(f32[128,128]{1,0:T(8,128)} %reduce-scatter.8.cloned.1.call-done) | copy-start | bytes 196612
Sparse Core Ops, SparseCore 0:
  48.7 19.2 reduce-scatter.3
  96.6 19.1 reduce-scatter.5
  177.4 18.4 reduce-scatter.7
where the time goes:
time: 243 us; the launch traced here: 242 us
  blocking collectives  82.9 us (34%)
  waiting for transfers between devices  68.4 us (28%)
  between operations  20.9 us (9%)
  other arithmetic  20.5 us (8%)
  starting transfers between devices  17.7 us (7%)
  matrix products  16.7 us (7%)
  local copies, waits for them, and re-layouts  14.9 us (6%)
    psum x2, blocking collectives, fold_sum(): folded = lax.psum((values[0], values[1]), ('seg', 'bin'))  65.3 us
    reduce_scatter x3, waiting for transfers between devices, reduce_rows(): lax.psum_scatter(partial_value, 'bin', scatter_dimension=0, tiled=True)  57.3 us
    ppermute x7, starting transfers between devices, from_behind(): return lax.ppermute(x, axis, pairs)  17.6 us
    scatter-add x6, other arithmetic, apply_local(): return summed.at[rows_low].add(own_term).at[rows_up].add(returned)  12.3 us
    all_gather x2, blocking collectives, spread(): whole_rows = lax.all_gather(vector, 'bin', axis=0, tiled=True)  11.6 us
    ppermute x7, waiting for transfers between devices, from_behind(): return lax.ppermute(x, axis, pairs)  11 us
    all_gather x1, blocking collectives, shards(): start_whole = lax.all_gather(start_factors, 'bin', axis=0, tiled=True)  5.97 us
  transfers between devices with their start and end apart: 10, of which 6 were waited for; matrix products, arithmetic and copies ran while one was open for 11% of the time, Pallas kernels for 0%

commit v1 on v0

--- a/solution.py
+++ b/solution.py
@@ -6,6 +6,10 @@
 ITERS = 2
 highest = lax.Precision.HIGHEST
 ridge_weight = 0.5
+
+
+def zone_order(patch):
+    return lax.psum(lax.psum(patch, "bin"), "seg")
 
 
 def from_behind(x, axis, by):
@@ -102,7 +106,7 @@
         return whole_rows
 
     def fold_sum(values):
-        folded = lax.psum((values[0], values[1]), ("seg", "bin"))
+        folded = zone_order((values[0], values[1]))
         return folded
 
     def image_of(vector):

time: 243 us -> 216 us (0.89)
  blocking collectives: 82.9 us -> 55.4 us
    psum x2 -> x4, blocking collectives: 65.3 us -> 37.8 us  [zone_order(): return lax.psum(lax.psum(patch, 'bin'), 'seg')]
  transfers between devices with their start and end apart: 10 -> 10, of which waited for: 6 -> 6; matrix products, arithmetic and copies ran while one was open for 11% -> 12% of each run, Pallas kernels for 0% -> 0%
where the time goes in v1:
time: 216 us; the launch traced here: 215 us
  waiting for transfers between devices  68.8 us (32%)
  blocking collectives  55.4 us (26%)
  between operations  20.9 us (10%)
  other arithmetic  20.4 us (9%)
  starting transfers between devices  17.7 us (8%)
  matrix products  16.7 us (8%)
  local copies, waits for them, and re-layouts  14.9 us (7%)
    reduce_scatter x3, waiting for transfers between devices, reduce_rows(): lax.psum_scatter(partial_value, 'bin', scatter_dimension=0, tiled=True)  57.7 us
    psum x4, blocking collectives, zone_order(): return lax.psum(lax.psum(patch, 'bin'), 'seg')  37.8 us
    ppermute x7, starting transfers between devices, from_behind(): return lax.ppermute(x, axis, pairs)  17.6 us
    scatter-add x6, other arithmetic, apply_local(): return summed.at[rows_low].add(own_term).at[rows_up].add(returned)  12.3 us
    all_gather x2, blocking collectives, spread(): whole_rows = lax.all_gather(vector, 'bin', axis=0, tiled=True)  11.6 us
    ppermute x7, waiting for transfers between devices, from_behind(): return lax.ppermute(x, axis, pairs)  11 us
    all_gather x1, blocking collectives, shards(): start_whole = lax.all_gather(start_factors, 'bin', axis=0, tiled=True)  5.97 us
  transfers between devices with their start and end apart: 10, of which 6 were waited for; matrix products, arithmetic and copies ran while one was open for 12% of the time, Pallas kernels for 0%

profile of v1, /device:TPU:0, one launch (start us, length us, event | category | flops | bytes accessed | tf_op | source)
XLA Modules:
  0.0 214.8 jit_solution(9673407274142111884)
XLA Ops:
  7.2 1.4 fusion.76
  8.6 5.6 %collective-permute-start = (s32[1]{0:T(128)}, s32[1]{0:T(128)}, u32[]{:S(2)}, u32[]{:S(2)}) collective-permute-start(s32[1]{0:T(128)} %bitcast.23), channel_id=1, source_target_pairs={{0,4},{4,8},{8,12},{1,5},{5,9},{9,13},{2,6},{6,10},{10,14},{3,7},{... | collective-permute-start | bytes 20 | tf_op jit(solution)/shard_map/ppermute | solution.py:18
  14.2 6.0 %all_gather.9 = f32[512,128]{1,0:T(8,128)S(1)} all-gather(f32[128,128]{1,0:T(8,128)} %param.11), channel_id=1, replica_groups=mesh['groups'=2,'seg'=4,'bin'=4] {'bin'}, dimensions={0}, use_global_device_ids=true | all-gather | bytes 327680 | tf_op jit(solution)/shard_map/all_gather | solution.py:115
  20.2 0.7 compare_convert_fusion
  20.9 0.7 gather_fusion.5
  21.7 3.0 %collective-permute-start.1 = (f32[256,128]{1,0:T(8,128)S(1)}, f32[256,128]{1,0:T(8,128)S(1)}, u32[]{:S(2)}, u32[]{:S(2)}) collective-permute-start(f32[256,128]{1,0:T(8,128)S(1)} %broadcast_multiply_fusion.2), channel_id=1, source_target_pairs={{0,4},{4,8},{8,12},{1,5},{5,9},{9,13},{2,6},{6,10},{10,14},{3,7},{... | collective-permute-start | bytes 393224 | tf_op jit(solution)/shard_map/ppermute | solution.py:18
  25.5 0.6 gather_fusion.1
  26.1 0.6 gather_fusion
  27.1 1.0 convolution_multiply_fusion.3
  28.6 0.7 copy-done.10
  29.5 0.6 gather_fusion.2
  30.0 0.6 gather_fusion.3
  32.2 0.9 convolution_add_fusion.2
  33.7 0.7 compare_convert_fusion.2
  34.4 0.7 gather_fusion.4
  35.7 0.9 fusion.9
  36.6 0.6 compare_convert_fusion.1
  37.7 0.7 multiply_subtract_fusion.2
  38.4 1.3 collective-permute-start.2
  40.1 2.0 scatter_fusion
  42.2 3.6 %collective-permute-done.2 = f32[256,128]{1,0:T(8,128)S(1)} collective-permute-done((f32[256,128]{1,0:T(8,128)S(1)}, f32[256,128]{1,0:T(8,128)S(1)}, u32[]{:S(2)}, u32[]{:S(2)}) %collective-permute-start.2) | collective-permute-done | bytes 131104 | tf_op jit(solution)/shard_map/ppermute | solution.py:18
  45.8 2.0 scatter_fusion.1
  47.8 0.7 bitcast_subtract_fusion
  48.6 19.4 %reduce-scatter.4.cloned.1.call-done = f32[128,128]{1,0:T(8,128)} async-done(((f32[512,128]{1,0:T(8,128)}), f32[128,128]{1,0:T(8,128)}) %reduce-scatter.4.cloned.1.call-update) | async-done | bytes 65552 | tf_op jit(solution)/shard_map/reduce_scatter | solution.py:101
  68.0 0.8 multiply_subtract_fusion.5
  68.9 5.8 %all_gather.10 = f32[512,128]{1,0:T(8,128)S(1)} all-gather(f32[128,128]{1,0:T(8,128)S(1)} %multiply_subtract_fusion.5), channel_id=1, replica_groups=mesh['groups'=2,'seg'=4,'bin'=4] {'bin'}, dimensions={0}, use_global_device_ids=true | all-gather | bytes 327680 | tf_op jit(solution)/shard_map/all_gather | solution.py:105
  74.6 0.7 gather_fusion.10
  75.4 0.7 gather_fusion.9
  76.1 0.6 gather_fusion.7
  76.7 0.6 gather_fusion.8
  77.2 0.6 gather_fusion.6
  78.6 3.6 %collective-permute-start.3 = (f32[256,128]{1,0:T(8,128)S(1)}, f32[256,128]{1,0:T(8,128)S(1)}, u32[]{:S(2)}, u32[]{:S(2)}) collective-permute-start(f32[256,128]{1,0:T(8,128)S(1)} %broadcast_multiply_fusion.1), channel_id=1, source_target_pairs={{0,4},{4,8},{8,12},{1,5},{5,9},{9,13},{2,6},{6,10},{10,14},{3,7},{... | collective-permute-start | bytes 393224 | tf_op jit(solution)/shard_map/ppermute | solution.py:18
  82.2 0.9 convolution_multiply_fusion.2
  84.2 0.9 convolution_add_fusion.1
  85.7 0.7 multiply_subtract_fusion.1
  86.4 1.3 collective-permute-start.4
  88.1 2.0 scatter_fusion.2
  90.2 3.6 %collective-permute-done.4 = f32[256,128]{1,0:T(8,128)S(1)} collective-permute-done((f32[256,128]{1,0:T(8,128)S(1)}, f32[256,128]{1,0:T(8,128)S(1)}, u32[]{:S(2)}, u32[]{:S(2)}) %collective-permute-start.4) | collective-permute-done | bytes 131104 | tf_op jit(solution)/shard_map/ppermute | solution.py:18
  93.7 2.0 scatter_fusion.3
  95.8 0.7 copy-done.2
  96.5 19.3 %reduce-scatter.6.cloned.1.call-done = f32[128,128]{1,0:T(8,128)} async-done(((f32[512,128]{1,0:T(8,128)}), f32[128,128]{1,0:T(8,128)}) %reduce-scatter.6.cloned.1.call-update) | async-done | bytes 65552 | tf_op jit(solution)/shard_map/reduce_scatter | solution.py:101
  115.9 1.5 multiply_reduce_fusion.2
  117.4 6.4 %all-reduce.1 = (f32[]{:T(128)}, f32[]{:T(128)}) all-reduce(f32[]{:T(128)} %get-tuple-element.9, f32[]{:T(128)} %get-tuple-element.8), channel_id=1, replica_groups=mesh['groups'=2,'seg'=4,'bin'=4] {'bin'}, use_global_device_ids=true, to_apply=%region_8.0 | all-reduce | flops 2 | bytes 16 | tf_op jit(solution)/shard_map/psum | solution.py:12
  123.8 12.5 %all-reduce.3 = (f32[]{:T(128)}, f32[]{:T(128)}) all-reduce(f32[]{:T(128)} %get-tuple-element.16, f32[]{:T(128)} %get-tuple-element.17), channel_id=1, replica_groups=mesh['groups'=2,'seg'=4,'bin'=4] {'seg'}, use_global_device_ids=true, to_apply=%region_9.0 | all-reduce | flops 2 | bytes 16 | tf_op jit(solution)/shard_map/psum | solution.py:12
  137.6 5.8 %all_gather.11 = f32[512,128]{1,0:T(8,128)S(1)} all-gather(f32[128,128]{1,0:T(8,128)S(1)} %multiply_subtract_fusion.4), channel_id=1, replica_groups=mesh['groups'=2,'seg'=4,'bin'=4] {'bin'}, dimensions={0}, use_global_device_ids=true | all-gather | bytes 327680 | tf_op jit(solution)/shard_map/all_gather | solution.py:105
  143.4 0.7 gather_fusion.15
  144.1 0.7 gather_fusion.14
  144.9 0.6 gather_fusion.12
  145.4 0.6 gather_fusion.13
  146.0 0.6 gather_fusion.11
  147.4 1.3 collective-permute-start.5
  148.7 0.9 convolution_multiply_fusion.1
  150.7 0.9 convolution_add_fusion
  152.2 0.7 multiply_subtract_fusion
  152.9 1.5 collective-permute-start.6
  154.8 2.0 scatter_fusion.4
  156.9 3.8 %collective-permute-done.6 = f32[256,128]{1,0:T(8,128)S(1)} collective-permute-done((f32[256,128]{1,0:T(8,128)S(1)}, f32[256,128]{1,0:T(8,128)S(1)}, u32[]{:S(2)}, u32[]{:S(2)}) %collective-permute-start.6) | collective-permute-done | bytes 131104 | tf_op jit(solution)/shard_map/ppermute | solution.py:18
  160.7 2.0 scatter_fusion.5
  162.7 0.7 copy-done.1
  163.4 19.0 %reduce-scatter.8.cloned.1.call-done = f32[128,128]{1,0:T(8,128)} async-done(((f32[512,128]{1,0:T(8,128)}), f32[128,128]{1,0:T(8,128)}) %reduce-scatter.8.cloned.1.call-update) | async-done | bytes 65552 | tf_op jit(solution)/shard_map/reduce_scatter | solution.py:101
  182.5 1.6 multiply_reduce_fusion
  184.1 6.4 %all-reduce = (f32[]{:T(128)}, f32[]{:T(128)}) all-reduce(f32[]{:T(128)} %get-tuple-element.7, f32[]{:T(128)} %get-tuple-element.6), channel_id=1, replica_groups=mesh['groups'=2,'seg'=4,'bin'=4] {'bin'}, use_global_device_ids=true, to_apply=%region_17.0 | all-reduce | flops 2 | bytes 16 | tf_op jit(solution)/shard_map/psum | solution.py:12
  190.5 12.5 %all-reduce.2 = (f32[]{:T(128)}, f32[]{:T(128)}) all-reduce(f32[]{:T(128)} %get-tuple-element.14, f32[]{:T(128)} %get-tuple-element.15), channel_id=1, replica_groups=mesh['groups'=2,'seg'=4,'bin'=4] {'seg'}, use_global_device_ids=true, to_apply=%region_18.0 | all-reduce | flops 2 | bytes 16 | tf_op jit(solution)/shard_map/psum | solution.py:12
  207.6 0.7 multiply_subtract_fusion.3
  (70 shorter events, 10.7 us)
Async XLA Ops:
  7.2 18.9 %copy-start = (bf16[1024,128]{1,0:T(8,128)(2,1)S(1)}, bf16[1024,128]{1,0:T(8,128)(2,1)}, u32[]{:S(2)}) copy-start(bf16[1024,128]{1,0:T(8,128)(2,1)} %param.12) | copy-start | bytes 786436
  7.2 60.8 %reduce-scatter.4.cloned.1.call-start = ((), (), s32[]{:S(2)}) async-start(), calls=%async_computation.3 | async-start | bytes 327680 | tf_op jit(solution)/shard_map/reduce_scatter | solution.py:101
  8.6 11.6 %copy-start.11 = (s32[1,1,2,256]{3,2,1,0:T(2,128)S(1)}, s32[1,1,2,256]{3,2,1,0:T(2,128)}, u32[]{:S(2)}) copy-start(s32[1,1,2,256]{3,2,1,0:T(2,128)} %param.19) | copy-start | bytes 6148
  8.6 28.0 %collective-permute-start = (s32[1]{0:T(128)}, s32[1]{0:T(128)}, u32[]{:S(2)}, u32[]{:S(2)}) collective-permute-start(s32[1]{0:T(128)} %bitcast.23), channel_id=1, source_target_pairs={{0,4},{4,8},{8,12},{1,5},{5,9},{9,13},{2,6},{6,10},{10,14},{3,7},{... | collective-permute-start | bytes 20 | tf_op jit(solution)/shard_map/ppermute | solution.py:18
  21.7 3.0 %copy-start.12 = (s32[1,1,12,2]{2,3,1,0:T(2,128)S(1)}, s32[1,1,12,2]{2,3,1,0:T(2,128)}, u32[]{:S(2)}) copy-start(s32[1,1,12,2]{2,3,1,0:T(2,128)} %param.15) | copy-start | bytes 292
  21.7 16.0 %collective-permute-start.1 = (f32[256,128]{1,0:T(8,128)S(1)}, f32[256,128]{1,0:T(8,128)S(1)}, u32[]{:S(2)}, u32[]{:S(2)}) collective-permute-start(f32[256,128]{1,0:T(8,128)S(1)} %broadcast_multiply_fusion.2), channel_id=1, source_target_pairs={{0,4},{4,8},{8,12},{1,5},{5,9},{9,13},{2,6},{6,10},{10,14},{3,7},{... | collective-permute-start | bytes 393224 | tf_op jit(solution)/shard_map/ppermute | solution.py:18
  26.1 1.0 copy-start.5
  28.5 0.7 copy-start.10
  30.0 0.9 copy-start.4
  34.4 1.0 copy-start.8
  36.6 1.0 copy-start.3
  38.4 7.4 %collective-permute-start.2 = (f32[256,128]{1,0:T(8,128)S(1)}, f32[256,128]{1,0:T(8,128)S(1)}, u32[]{:S(2)}, u32[]{:S(2)}) collective-permute-start(f32[256,128]{1,0:T(8,128)S(1)} %multiply_subtract_fusion.2), channel_id=1, source_target_pairs={{4,0},{8,4},{12,8},{5,1},{9,5},{13,9},{6,2},{10,6},{14,10},{7,3},{... | collective-permute-start | bytes 393224 | tf_op jit(solution)/shard_map/ppermute | solution.py:18
  48.5 19.5 %copy-start.6 = (f32[128,128]{1,0:T(8,128)S(1)}, f32[128,128]{1,0:T(8,128)}, u32[]{:S(2)}) copy-start(f32[128,128]{1,0:T(8,128)} %param.11) | copy-start | bytes 196612
  48.6 67.3 %reduce-scatter.6.cloned.1.call-start = ((), (), s32[]{:S(2)}) async-start(), calls=%async_computation.4 | async-start | bytes 327680 | tf_op jit(solution)/shard_map/reduce_scatter | solution.py:101
  78.6 7.1 %collective-permute-start.3 = (f32[256,128]{1,0:T(8,128)S(1)}, f32[256,128]{1,0:T(8,128)S(1)}, u32[]{:S(2)}, u32[]{:S(2)}) collective-permute-start(f32[256,128]{1,0:T(8,128)S(1)} %broadcast_multiply_fusion.1), channel_id=1, source_target_pairs={{0,4},{4,8},{8,12},{1,5},{5,9},{9,13},{2,6},{6,10},{10,14},{3,7},{... | collective-permute-start | bytes 393224 | tf_op jit(solution)/shard_map/ppermute | solution.py:18
  86.4 7.4 %collective-permute-start.4 = (f32[256,128]{1,0:T(8,128)S(1)}, f32[256,128]{1,0:T(8,128)S(1)}, u32[]{:S(2)}, u32[]{:S(2)}) collective-permute-start(f32[256,128]{1,0:T(8,128)S(1)} %multiply_subtract_fusion.1), channel_id=1, source_target_pairs={{4,0},{8,4},{12,8},{5,1},{9,5},{13,9},{6,2},{10,6},{14,10},{7,3},{... | collective-permute-start | bytes 393224 | tf_op jit(solution)/shard_map/ppermute | solution.py:18
  95.8 0.7 copy-start.2
  96.5 86.0 %reduce-scatter.8.cloned.1.call-start = ((), (), s32[]{:S(2)}) async-start(), calls=%async_computation.5 | async-start | bytes 327680 | tf_op jit(solution)/shard_map/reduce_scatter | solution.py:101
  115.8 21.7 %copy-start.7 = (f32[128,128]{1,0:T(8,128)S(1)}, f32[128,128]{1,0:T(8,128)}, u32[]{:S(2)}) copy-start(f32[128,128]{1,0:T(8,128)} %reduce-scatter.6.cloned.1.call-done) | copy-start | bytes 196612
  147.4 4.8 %collective-permute-start.5 = (f32[256,128]{1,0:T(8,128)S(1)}, f32[256,128]{1,0:T(8,128)S(1)}, u32[]{:S(2)}, u32[]{:S(2)}) collective-permute-start(f32[256,128]{1,0:T(8,128)S(1)} %broadcast_multiply_fusion), channel_id=1, source_target_pairs={{0,4},{4,8},{8,12},{1,5},{5,9},{9,13},{2,6},{6,10},{10,14},{3,7},{... | collective-permute-start | bytes 393224 | tf_op jit(solution)/shard_map/ppermute | solution.py:18
  152.9 7.8 %collective-permute-start.6 = (f32[256,128]{1,0:T(8,128)S(1)}, f32[256,128]{1,0:T(8,128)S(1)}, u32[]{:S(2)}, u32[]{:S(2)}) collective-permute-start(f32[256,128]{1,0:T(8,128)S(1)} %multiply_subtract_fusion), channel_id=1, source_target_pairs={{4,0},{8,4},{12,8},{5,1},{9,5},{13,9},{6,2},{10,6},{14,10},{7,3},{... | collective-permute-start | bytes 393224 | tf_op jit(solution)/shard_map/ppermute | solution.py:18
  162.7 0.7 copy-start.1
  182.5 25.2 %copy-start.9 = (f32[128,128]{1,0:T(8,128)S(1)}, f32[128,128]{1,0:T(8,128)}, u32[]{:S(2)}) copy-start(f32[128,128]{1,0:T(8,128)} %reduce-scatter.8.cloned.1.call-done) | copy-start | bytes 196612
Sparse Core Ops, SparseCore 0:
  48.7 19.2 reduce-scatter.3
  96.6 19.1 reduce-scatter.5
  163.6 18.8 reduce-scatter.7
